TPU v7x, 32 devices: a whole 2x2x4 slice. The times are simulated.
32 devices in a mesh: blk: 16 (over z, x, core), cuts: 2 (over y).
Axes of the slice: x: 2, y: 2, z: 4, core: 2. Of those that a mesh axis runs over, the one named last changes fastest.
Arguments:
- left_env: bfloat16 [2048, 8, 2048], P('blk', 'cuts'), may hold values from -4 to 4
- right_env: bfloat16 [2048, 8, 2048], P('blk', 'cuts'), may hold values from -4 to 4
- left_core: float32 [8, 8, 2, 2], replicated, may hold values from -1.5 to 1.5
- right_core: float32 [8, 8, 2, 2], replicated, may hold values from -1.5 to 1.5
- slot_bond: int32 [8], replicated, may hold values from 0 to 7, each once
- krylov_basis: float32 [8, 2048, 4, 2048], P(None, 'blk', None, 'cuts'), may hold values from -30 to 30
- beta_prev: float32 [], replicated, may hold values from 0.3 to 1.2
Outputs:
- next_vector: float32 [2048, 4, 2048], P('blk', None, 'cuts')
- alpha_values: float32 [1], replicated
- beta_values: float32 [1], replicated
Inputs may be any that keep to these rules, and one draw needn't show every extreme that they name: `slot_bond`: a permutation of the 8 bond values.
All inputs are finite; a program needn't handle non-finite values.
Results may differ from a plain program's by a relative error of at most 0.00073.
The roundings to bfloat16 on the way count: a program that leaves them out, or rounds other values in their place, can miss the bound.
Values may be sent and summed in bfloat16 or wider, within the bound.
No kernel may reach another device: no remote copies, remote signals or barrier semaphores. Data moves between devices by JAX's collectives and lax.ppermute only.
A program may use at most 192 MiB of HBM per device.

v0:
```python
import jax
import jax.numpy as jnp
from jax import lax
from jax.sharding import PartitionSpec as P


def build_table(left_core, right_core, slot_bond):
    bond_width = left_core.shape[0]
    phys_dim = left_core.shape[2]
    chosen = (slot_bond[:, None] == jnp.arange(bond_width, dtype=jnp.int32)[None, :]).astype(
        jnp.float32
    )
    picked = jnp.einsum("kw,wxac->kxac", chosen, left_core, precision=lax.Precision.HIGHEST)
    table = jnp.einsum("kxac,xybd->kyabcd", picked, right_core, precision=lax.Precision.HIGHEST)
    return table.reshape(bond_width, bond_width, phys_dim * phys_dim, phys_dim * phys_dim)


def on_device(left_env, right_env, left_core, right_core, slot_bond, krylov_basis, beta_prev):
    highest = lax.Precision.HIGHEST
    bond_width = left_core.shape[0]
    pair_count = left_core.shape[2] * left_core.shape[2]
    basis_count = krylov_basis.shape[0]
    row_count = krylov_basis.shape[1]
    col_count = krylov_basis.shape[3]
    full_width = left_env.shape[2]
    entries = float(full_width * pair_count * full_width)
    mpo_table = build_table(left_core, right_core, slot_bond)
    left_full = lax.all_gather(left_env, "cuts", axis=1, tiled=True)
    left_matrix = left_full.reshape(row_count * bond_width, full_width)
    right_local = lax.all_to_all(right_env, "cuts", split_axis=2, concat_axis=1, tiled=True)
    next_vector = krylov_basis[basis_count - 1]
    current_f = krylov_basis[basis_count - 1]
    previous = krylov_basis[basis_count - 2]
    current = current_f.astype(jnp.bfloat16)
    block_rows = lax.all_gather(current, "blk", axis=0, tiled=True)
    count_rows = block_rows.shape[0]
    projected = jnp.dot(
        left_matrix,
        block_rows.reshape(count_rows, pair_count * col_count),
        preferred_element_type=jnp.float32,
    )
    projected = projected.reshape(row_count, bond_width, pair_count, col_count)
    mixed_left = jnp.einsum("kypq,akqb->apyb", mpo_table, projected, precision=highest).astype(
        jnp.bfloat16
    )
    left_side = mixed_left.reshape(row_count * pair_count, bond_width * col_count)
    block_rows = lax.all_gather(right_local, "blk", axis=0, tiled=True)
    flat_rows = block_rows.reshape(block_rows.shape[0], -1)
    partial_terms = lax.dot_general(
        left_side, flat_rows, (((1,), (1,)), ((), ())), preferred_element_type=jnp.float32
    )
    image_vec = lax.psum_scatter(
        partial_terms.reshape(row_count, pair_count, full_width),
        "cuts",
        scatter_dimension=2,
        tiled=True,
    )
    local_gram = jnp.einsum("japb,kapb->jk", krylov_basis, krylov_basis, precision=highest)
    gram_matrix = lax.psum(local_gram, ("blk", "cuts")) / entries
    local_prods = jnp.einsum("japb,apb->j", krylov_basis, image_vec, precision=highest)
    inner_prods, image_square = lax.psum(
        (local_prods, jnp.sum(image_vec * image_vec)), ("blk", "cuts")
    )
    inner_prods = inner_prods / entries
    image_square = image_square / entries
    alpha_now = inner_prods[basis_count - 1]
    ortho_coeffs = (
        inner_prods
        - alpha_now * gram_matrix[:, basis_count - 1]
        - beta_prev * gram_matrix[:, basis_count - 2]
    )
    first_square = (
        image_square
        - 2.0 * alpha_now * inner_prods[basis_count - 1]
        - 2.0 * beta_prev * inner_prods[basis_count - 2]
        + alpha_now * alpha_now * gram_matrix[basis_count - 1, basis_count - 1]
        + 2.0 * alpha_now * beta_prev * gram_matrix[basis_count - 1, basis_count - 2]
        + beta_prev * beta_prev * gram_matrix[basis_count - 2, basis_count - 2]
    )
    square_mean = (
        first_square
        - 2.0 * jnp.sum(ortho_coeffs * ortho_coeffs)
        + jnp.sum(ortho_coeffs[:, None] * gram_matrix * ortho_coeffs[None, :])
    )
    first_pass = image_vec - alpha_now * current_f - beta_prev * previous
    second_pass = first_pass - jnp.einsum(
        "j,japb->apb", ortho_coeffs, krylov_basis, precision=highest
    )
    beta_new = jnp.sqrt(square_mean + 1e-06)
    next_vector = second_pass / beta_new
    alpha_list = [alpha_now]
    beta_list = [beta_new]
    return (next_vector, jnp.stack(alpha_list), jnp.stack(beta_list))


def solution(mesh):
    in_specs = (
        P("blk", "cuts", None),
        P("blk", "cuts", None),
        P(),
        P(),
        P(),
        P(None, "blk", None, "cuts"),
        P(),
    )
    out_specs = (P("blk", None, "cuts"), P(), P())
    return jax.shard_map(
        on_device, mesh=mesh, in_specs=in_specs, out_specs=out_specs, check_vma=False
    )
```

profile of v0, /device:TPU:0, one launch (start us, length us, event | category | flops | bytes accessed | tf_op | source)
XLA Modules:
  0.0 616.2 jit_solution(4557364010513093199)
XLA Ops:
  7.2 0.0 copy-start
  7.2 0.0 all-gather.9.cloned.1.call-start
  7.2 4.5 fusion.43
  11.7 0.0 copy-start.3
  11.7 0.0 copy-start.4
  11.7 1.3 copy-done.3
  13.1 2.1 copy.113
  15.2 0.0 all-gather.9.cloned.1.call-update
  15.2 0.0 all-gather.5.cloned.1.call-start
  15.2 0.0 copy-done.4
  15.2 2.5 copy.42
  17.7 0.0 all-gather.5.cloned.1.call-update
  17.8 0.0 all-gather.7.cloned.1.call-start
  17.8 5.6 copy.50
  23.4 30.2 %all_to_all.18 = bf16[128,4,2048]{0,1,2:T(4,128)(2,1)S(1)} all-to-all(bf16[128,4,2048]{0,1,2:T(4,128)(2,1)} %copy.50), channel_id=1, replica_groups=mesh['blk'=16,'cuts'=2] {'cuts'}, dimensions={2} | all-to-all | bytes 4194304 | tf_op jit(solution)/shard_map/all_to_all | solution.py:30
  53.6 0.0 copy-start.6
  53.6 0.0 copy-start.7
  53.6 2.7 copy.51
  56.3 0.0 all-gather.7.cloned.1.call-update
  56.3 0.0 reduce-scatter.2.cloned.1.call-start
  56.3 0.0 copy-done.6
  56.3 0.0 copy-done.7
  56.4 0.2 convolution_bitcast_fusion.1
  56.5 0.0 copy-done
  56.5 0.2 convolution_bitcast_fusion
  56.7 0.6 copy.48
  57.4 87.1 %all-gather.9.cloned.1.call-done = bf16[1,2048,4,1024]{3,1,2,0:T(8,128)(2,1)} async-done(((bf16[1,128,4,1024]{3,1,2,0:T(8,128)(2,1)}), bf16[1,2048,4,1024]{3,1,2,0:T(8,128)(2,1)}) %all-gather.9.cloned.1.call-update) | async-done | bytes 16777232 | tf_op jit(solution)/shard_map/all_gather | solution.py:35
  144.5 22.2 %copy.44 = bf16[1,2048,4,1024]{1,3,2,0:T(8,128)(2,1)} copy(bf16[1,2048,4,1024]{3,1,2,0:T(8,128)(2,1)} %all-gather.9.cloned.1.call-done) | data formatting | bytes 33554432 | tf_op jit(solution)/shard_map/all_gather | solution.py:35
  166.7 34.2 %all-gather.5.cloned.1.call-done = bf16[128,8,2048]{2,0,1:T(8,128)(2,1)} async-done(((bf16[128,4,2048]{2,0,1:T(8,128)(2,1)}), bf16[128,8,2048]{2,0,1:T(8,128)(2,1)}) %all-gather.5.cloned.1.call-update) | async-done | bytes 4194320 | tf_op jit(solution)/shard_map/all_gather | solution.py:28
  201.0 0.0 copy-start.5
  201.0 25.6 %fusion.4 = f32[128,8,4,1024]{3,1,2,0:T(8,128)} fusion(bf16[1,2048,4,1024]{1,3,2,0:T(8,128)(2,1)} %copy.44, bf16[128,8,2048,1]{2,0,1,3:T(8,128)(2,1)} %bitcast.94), kind=kOutput, calls=%fused_computation.4 | convolution fusion | flops 17179869184 | bytes 37748736 | tf_op jit(solution)/shard_map/dot_general | solution.py:37
  226.6 0.0 copy-done.5
  226.6 20.6 %fusion.15 = bf16[128,4,8,1024]{3,2,1,0:T(8,128)(2,1)} fusion(f32[8,8,4,4,1]{1,0,3,2,4:T(8,128)S(1)} %bitcast.93, f32[128,8,4,1024]{3,1,2,0:T(8,128)} %fusion.4), kind=kOutput, calls=%fused_computation.14 | convolution fusion | flops 1614807040 | bytes 25169920 | tf_op jit(solution)/shard_map/kypq,akqb->apyb/dot_general | solution.py:43
  247.2 123.4 %all-gather.7.cloned.1.call-done = bf16[2048,8,1024]{2,0,1:T(8,128)(2,1)} async-done(((bf16[128,8,1024]{2,0,1:T(8,128)(2,1)}), bf16[2048,8,1024]{2,0,1:T(8,128)(2,1)}) %all-gather.7.cloned.1.call-update) | async-done | bytes 33554448 | tf_op jit(solution)/shard_map/all_gather | solution.py:47
  370.6 46.7 %fusion.19 = f32[128,4,2048]{2,0,1:T(8,128)} fusion(bf16[2048,8,1024]{2,0,1:T(8,128)(2,1)} %all-gather.7.cloned.1.call-done, bf16[128,4,8,1024]{3,2,1,0:T(8,128)(2,1)} %fusion.15), kind=kOutput, calls=%fused_computation.16 | convolution fusion | flops 17179869184 | bytes 46137344 | tf_op jit(solution)/shard_map/dot_general | solution.py:49
  417.3 0.0 reduce-scatter.2.cloned.1.call-update
  418.0 54.5 %fusion.29 = f32[8,8]{1,0:T(8,128)S(1)} fusion(f32[8,128,4,1024]{3,2,1,0:T(4,128)} %param.12), kind=kOutput, calls=%fused_computation.28 | convolution fusion | flops 402653184 | bytes 16777472 | tf_op jit(solution)/shard_map/japb,kapb->jk/dot_general | solution.py:58
  472.5 0.0 reduce-scatter.2.cloned.1.call-done
  472.5 0.0 copy-start.2
  472.5 43.3 %fusion.32 = f32[8]{0:T(128)S(1)} fusion(f32[8,128,4,1024]{3,2,1,0:T(4,128)} %param.12, f32[128,4,1024,1]{2,0,1,3:T(8,128)} %bitcast.90), kind=kOutput, calls=%fused_computation.29 | convolution fusion | flops 50331648 | bytes 18874400 | tf_op jit(solution)/shard_map/japb,apb->j/dot_general | solution.py:60
  515.8 0.0 copy-done.2
  515.8 1.1 multiply_reduce_fusion
  517.0 39.9 %all-reduce = (f32[8,8]{1,0:T(8,128)S(1)}, f32[8]{0:T(128)S(1)}, f32[]{:T(128)}) all-reduce(f32[8,8]{1,0:T(8,128)S(1)} %fusion.29, f32[8]{0:T(128)S(1)} %fusion.32, f32[]{:T(128)} %multiply_reduce_fusion), channel_id=1, replica_groups=mesh['blk'=16,'cuts'=2] {'blk','cuts'}, use_global_device_ids=true, to_apply=%region_2.0 | all-reduce | flops 73 | bytes 584 | tf_op jit(solution)/shard_map/psum | solution.py:59
  556.9 0.6 fusion.45
  559.5 0.9 multiply_reduce_fusion.3
  560.3 0.7 fusion.44
  561.7 0.7 multiply_reduce_fusion.4
  562.3 30.8 %fusion.6 = f32[1,128,4,1024]{3,0,2,1:T(1,128)} fusion(f32[8,128,4,1024]{3,2,1,0:T(4,128)} %param.12, f32[8]{0:T(128)S(1)} %get-tuple-element.21), kind=kOutput, calls=%fused_computation.7 | convolution fusion | flops 50331648 | bytes 18874400 | tf_op jit(solution)/shard_map/j,japb->apb/dot_general | solution.py:86
  593.1 0.7 multiply_reduce_fusion.1
  598.4 0.0 copy-start.1
  598.4 6.9 %fusion.27 = f32[128,4,1024]{2,0,1:T(8,128)S(1)} fusion(f32[1,128,4,1024]{3,2,1,0:T(4,128)} %get-tuple-element.23, f32[128,4,1024]{2,0,1:T(8,128)S(1)} %copy-done.2, f32[1,128,4,1024]{3,0,2,1:T(1,128)} %fusion.6, f32[1,128,4,1024]{3,2,1,0:T(4,128)} %copy-done.3, f32[]{:T(128)} %sqrt.3, f32[]{:T(128)S(6)} %copy.114, f32[]{:T(128)} %bitcast.27), kind=kLoop, calls=%fused_computation.21 | loop fusion | flops 3145728 | bytes 10485772 | tf_op jit(solution)/shard_map/div | solution.py:90
  605.3 2.7 copy.56
  608.0 0.0 copy-done.1
  (3 shorter events, 0.0 us)
Async XLA Ops:
  7.2 49.4 %copy-start = (f32[8,8,2,2]{1,3,2,0:T(2,128)S(1)}, f32[8,8,2,2]{1,3,2,0:T(2,128)}, u32[]{:S(2)}) copy-start(f32[8,8,2,2]{1,3,2,0:T(2,128)} %param.10) | copy-start | bytes 3076
  7.2 137.3 %all-gather.9.cloned.1.call-start = ((), (), s32[]{:S(2)}) async-start(), calls=%async_computation.5 | async-start | bytes 17825792 | tf_op jit(solution)/shard_map/all_gather | solution.py:35
  11.7 1.3 copy-start.3
  11.7 3.5 copy-start.4
  15.2 185.8 %all-gather.5.cloned.1.call-start = ((), (), s32[]{:S(2)}) async-start(), calls=%async_computation.2 | async-start | bytes 6291456 | tf_op jit(solution)/shard_map/all_gather | solution.py:28
  17.8 352.9 %all-gather.7.cloned.1.call-start = ((), (), s32[]{:S(2)}) async-start(), calls=%async_computation.3 | async-start | bytes 35651584 | tf_op jit(solution)/shard_map/all_gather | solution.py:47
  53.6 2.8 copy-start.6
  53.6 2.8 copy-start.7
  56.3 416.2 %reduce-scatter.2.cloned.1.call-start = ((), (), s32[]{:S(2)}) async-start(), calls=%async_computation.4 | async-start | bytes 6291456 | tf_op jit(solution)/shard_map/reduce_scatter | solution.py:52
  201.0 25.6 %copy-start.5 = (f32[8,8,2,2,2,2]{1,0,5,4,3,2:T(8,128)S(1)}, f32[8,8,2,2,2,2]{1,0,5,4,3,2:T(8,128)}, u32[]{:S(2)}) copy-start(f32[8,8,2,2,2,2]{1,0,5,4,3,2:T(8,128)} %copy.48) | copy-start | bytes 12292
  472.5 43.3 %copy-start.2 = (f32[128,4,1024]{2,0,1:T(8,128)S(1)}, f32[128,4,1024]{2,0,1:T(8,128)}, u32[]{:S(2)}) copy-start(f32[128,4,1024]{2,0,1:T(8,128)} %reduce-scatter.2.cloned.1.call-done) | copy-start | bytes 6291460
  598.4 9.6 %copy-start.1 = (f32[8,8,2,2]{1,3,2,0:T(2,128)S(1)}, f32[8,8,2,2]{1,3,2,0:T(2,128)}, u32[]{:S(2)}) copy-start(f32[8,8,2,2]{1,3,2,0:T(2,128)} %param.10) | copy-start | bytes 3076
Sparse Core Ops, SparseCore 0:
  15.3 129.1 all-gather.8
  146.0 54.8 all-gather.4
  202.5 168.0 all-gather.6
  417.5 54.3 reduce-scatter.1
where the time goes:
time: 624 us; the launch traced here: 616 us
  waiting for transfers between devices  245 us (39%)
  matrix products  222 us (36%)
  blocking collectives  70.2 us (11%)
  local copies, waits for them, and re-layouts  45.5 us (7%)
  between operations  23.3 us (4%)
  other arithmetic  10.3 us (2%)
    all_gather x1, waiting for transfers between devices, on_device(): block_rows = lax.all_gather(right_local, 'blk', axis=0, tiled=True)  123 us
    all_gather x1, waiting for transfers between devices, on_device(): block_rows = lax.all_gather(current, 'blk', axis=0, tiled=True)  87.1 us
    dot_general x1, matrix products, on_device(): jnp.einsum('japb,kapb->jk', krylov_basis, krylov_basis, precision=highest)  54.5 us
    dot_general x1, matrix products, on_device(): lax.dot_general(left_side, flat_rows, (((1,), (1,)), ((), ())), preferred...  46.7 us
    dot_general x1, matrix products, on_device(): jnp.einsum('japb,apb->j', krylov_basis, image_vec, precision=highest)  43.3 us
    psum x1, blocking collectives, on_device(): gram_matrix = lax.psum(local_gram, ('blk', 'cuts')) / entries  39.9 us
    all_gather x1, waiting for transfers between devices, on_device(): left_full = lax.all_gather(left_env, 'cuts', axis=1, tiled=True)  34.2 us
    dot_general x1, matrix products, on_device(): jnp.einsum('j,japb->apb', ortho_coeffs, krylov_basis, precision=highest)  30.8 us
  transfers between devices with their start and end apart: 4, of which 3 were waited for; matrix products, arithmetic and copies ran while one was open for 22% of the time, Pallas kernels for 0%

commit v1 on v0

--- a/solution.py
+++ b/solution.py
@@ -25,18 +25,39 @@
     full_width = left_env.shape[2]
     entries = float(full_width * pair_count * full_width)
     mpo_table = build_table(left_core, right_core, slot_bond)
-    left_full = lax.all_gather(left_env, "cuts", axis=1, tiled=True)
-    left_matrix = left_full.reshape(row_count * bond_width, full_width)
-    right_local = lax.all_to_all(right_env, "cuts", split_axis=2, concat_axis=1, tiled=True)
-    next_vector = krylov_basis[basis_count - 1]
+    cut_count = lax.axis_size("cuts")
+    cut_index = lax.axis_index("cuts")
+    paired = cut_count == 2
+    swap = [(0, 1), (1, 0)]
     current_f = krylov_basis[basis_count - 1]
-    previous = krylov_basis[basis_count - 2]
     current = current_f.astype(jnp.bfloat16)
     block_rows = lax.all_gather(current, "blk", axis=0, tiled=True)
-    count_rows = block_rows.shape[0]
+    if paired:
+        half = left_env.shape[1]
+        left_full = jnp.concatenate([left_env, lax.ppermute(left_env, "cuts", swap)], axis=1)
+        kept = lax.dynamic_slice_in_dim(right_env, cut_index * col_count, col_count, 2)
+        sent = lax.dynamic_slice_in_dim(right_env, (1 - cut_index) * col_count, col_count, 2)
+        right_local = jnp.concatenate([kept, lax.ppermute(sent, "cuts", swap)], axis=1)
+        turned = jnp.roll(mpo_table, (half, half), axis=(0, 1))
+        mpo_table = jnp.where(cut_index == 0, mpo_table, turned)
+    else:
+        left_full = lax.all_gather(left_env, "cuts", axis=1, tiled=True)
+        right_local = lax.all_to_all(right_env, "cuts", split_axis=2, concat_axis=1, tiled=True)
+    local_gram = jnp.einsum("japb,kapb->jk", krylov_basis, krylov_basis, precision=highest)
+    right_rows = right_local.shape[0]
+    chunk_count = 2 if paired and right_rows % 32 == 0 else 1
+    chunk_rows = right_rows // chunk_count
+    chunks = [
+        right_local[index * chunk_rows : (index + 1) * chunk_rows] for index in range(chunk_count)
+    ]
+    chunks, block_rows, left_full, local_gram = lax.optimization_barrier(
+        (chunks, block_rows, left_full, local_gram)
+    )
+    gathered = [lax.all_gather(chunk, "blk", axis=0, tiled=True) for chunk in chunks]
+    left_matrix = left_full.reshape(row_count * bond_width, full_width)
     projected = jnp.dot(
         left_matrix,
-        block_rows.reshape(count_rows, pair_count * col_count),
+        block_rows.reshape(block_rows.shape[0], pair_count * col_count),
         preferred_element_type=jnp.float32,
     )
     projected = projected.reshape(row_count, bond_width, pair_count, col_count)
@@ -44,23 +65,29 @@
         jnp.bfloat16
     )
     left_side = mixed_left.reshape(row_count * pair_count, bond_width * col_count)
-    block_rows = lax.all_gather(right_local, "blk", axis=0, tiled=True)
-    flat_rows = block_rows.reshape(block_rows.shape[0], -1)
-    partial_terms = lax.dot_general(
-        left_side, flat_rows, (((1,), (1,)), ((), ())), preferred_element_type=jnp.float32
+    pieces = []
+    for rows in gathered:
+        partial_terms = lax.dot_general(
+            left_side,
+            rows.reshape(rows.shape[0], -1),
+            (((1,), (1,)), ((), ())),
+            preferred_element_type=jnp.float32,
+        )
+        width = partial_terms.shape[1] // cut_count
+        partial_terms = partial_terms.reshape(row_count, pair_count, cut_count * width)
+        if paired:
+            own = lax.dynamic_slice_in_dim(partial_terms, cut_index * width, width, 2)
+            other = lax.dynamic_slice_in_dim(partial_terms, (1 - cut_index) * width, width, 2)
+            piece = own + lax.ppermute(other, "cuts", swap)
+        else:
+            piece = lax.psum_scatter(partial_terms, "cuts", scatter_dimension=2, tiled=True)
+        pieces.append(piece.reshape(row_count, pair_count, width // chunk_rows, chunk_rows))
+    image_vec = jnp.concatenate(pieces, axis=3).reshape(row_count, pair_count, col_count)
+    local_prods = jnp.sum(krylov_basis * image_vec[None], axis=(1, 2, 3))
+    gram_matrix, inner_prods, image_square = lax.psum(
+        (local_gram, local_prods, jnp.sum(image_vec * image_vec)), ("blk", "cuts")
     )
-    image_vec = lax.psum_scatter(
-        partial_terms.reshape(row_count, pair_count, full_width),
-        "cuts",
-        scatter_dimension=2,
-        tiled=True,
-    )
-    local_gram = jnp.einsum("japb,kapb->jk", krylov_basis, krylov_basis, precision=highest)
-    gram_matrix = lax.psum(local_gram, ("blk", "cuts")) / entries
-    local_prods = jnp.einsum("japb,apb->j", krylov_basis, image_vec, precision=highest)
-    inner_prods, image_square = lax.psum(
-        (local_prods, jnp.sum(image_vec * image_vec)), ("blk", "cuts")
-    )
+    gram_matrix = gram_matrix / entries
     inner_prods = inner_prods / entries
     image_square = image_square / entries
     alpha_now = inner_prods[basis_count - 1]
@@ -82,12 +109,12 @@
         - 2.0 * jnp.sum(ortho_coeffs * ortho_coeffs)
         + jnp.sum(ortho_coeffs[:, None] * gram_matrix * ortho_coeffs[None, :])
     )
-    first_pass = image_vec - alpha_now * current_f - beta_prev * previous
-    second_pass = first_pass - jnp.einsum(
-        "j,japb->apb", ortho_coeffs, krylov_basis, precision=highest
-    )
     beta_new = jnp.sqrt(square_mean + 1e-06)
-    next_vector = second_pass / beta_new
+    weights = ortho_coeffs.at[basis_count - 1].add(alpha_now).at[basis_count - 2].add(beta_prev)
+    removed = weights[0] * krylov_basis[0]
+    for index in range(1, basis_count):
+        removed = removed + weights[index] * krylov_basis[index]
+    next_vector = (image_vec - removed) / beta_new
     alpha_list = [alpha_now]
     beta_list = [beta_new]
     return (next_vector, jnp.stack(alpha_list), jnp.stack(beta_list))

time: 624 us -> 540 us (0.87)
  matrix products: 222 us -> 170 us
  waiting for transfers between devices: 245 us -> 207 us
  blocking collectives: 70.2 us -> 38.6 us
  other arithmetic: 10.3 us -> 34.4 us
  local copies, waits for them, and re-layouts: 45.5 us -> 55.6 us
    dot_general x4 -> x3, matrix products: 146 us -> 93 us  [the longest x2 69.3 us: on_device(): lax.dot_general(left_side, rows.reshape(rows.shape[0], -1), (((1,), (1,))...]
    all_gather x1, waiting for transfers between devices: 87.1 us -> 50.7 us  [on_device(): block_rows = lax.all_gather(current, 'blk', axis=0, tiled=True)]
    all_gather x2, waiting for transfers between devices: 158 us -> 124 us  [on_device(): lax.all_gather(chunk, 'blk', axis=0, tiled=True)]
    ppermute x0 -> x4, waiting for transfers between devices: none -> 32.5 us  [the longest x2 21.4 us: on_device(): piece = own + lax.ppermute(other, 'cuts', swap)]
    all_to_all x1 -> x0, blocking collectives: 30.2 us -> none  [on_device(): lax.all_to_all(right_env, 'cuts', split_axis=2, concat_axis=1, tiled=True)]
    dot_general x0 -> x1, local copies, waits for them, and re-layouts: none -> 22.5 us  [on_device(): jnp.dot(left_matrix, block_rows.reshape(block_rows.shape[0], pair_count *...]
    all_gather x1 -> x0, local copies, waits for them, and re-layouts: 22.2 us -> none  [on_device(): block_rows = lax.all_gather(current, 'blk', axis=0, tiled=True)]
    reduce_sum x0 -> x1, other arithmetic: none -> 7.74 us  [on_device(): local_prods = jnp.sum(krylov_basis * image_vec[None], axis=(1, 2, 3))]
  transfers between devices with their start and end apart: 4 -> 7, of which waited for: 3 -> 5; matrix products, arithmetic and copies ran while one was open for 22% -> 42% of each run, Pallas kernels for 0% -> 0%
where the time goes in v1:
time: 540 us; the launch traced here: 536 us
  waiting for transfers between devices  207 us (38%)
  matrix products  170 us (31%)
  local copies, waits for them, and re-layouts  55.6 us (10%)
  blocking collectives  38.6 us (7%)
  other arithmetic  34.4 us (6%)
  between operations  25 us (5%)
  starting transfers between devices  6.3 us (1%)
    all_gather x2, waiting for transfers between devices, on_device(): lax.all_gather(chunk, 'blk', axis=0, tiled=True)  124 us
    dot_general x2, matrix products, on_device(): lax.dot_general(left_side, rows.reshape(rows.shape[0], -1), (((1,), (1,))...  69.3 us
    dot_general x1, matrix products, on_device(): jnp.einsum('japb,kapb->jk', krylov_basis, krylov_basis, precision=highest)  55.5 us
    all_gather x1, waiting for transfers between devices, on_device(): block_rows = lax.all_gather(current, 'blk', axis=0, tiled=True)  50.7 us
    psum x1, blocking collectives, on_device(): lax.psum((local_gram, local_prods, jnp.sum(image_vec * image_vec)), ('blk...  38.6 us
    dot_general x1, matrix products, on_device(): jnp.dot(left_matrix, block_rows.reshape(block_rows.shape[0], pair_count *...  23.7 us
    dot_general x1, local copies, waits for them, and re-layouts, on_device(): jnp.dot(left_matrix, block_rows.reshape(block_rows.shape[0], pair_count *...  22.5 us
    ppermute x2, waiting for transfers between devices, on_device(): piece = own + lax.ppermute(other, 'cuts', swap)  21.4 us
  transfers between devices with their start and end apart: 7, of which 5 were waited for; matrix products, arithmetic and copies ran while one was open for 42% of the time, Pallas kernels for 0%

profile of v1, /device:TPU:0, one launch (start us, length us, event | category | flops | bytes accessed | tf_op | source)
XLA Modules:
  0.0 536.3 jit_solution(16643390571547761057)
XLA Ops:
  7.2 0.0 copy-start
  7.2 0.0 all-gather.9.cloned.1.call-start
  7.2 3.2 bitcast_convert_fusion.1
  10.4 0.0 all-gather.9.cloned.1.call-update
  10.4 0.0 all-gather.5.cloned.1.call-start
  10.5 3.1 collective-permute-start.1
  13.5 0.0 copy-done.2
  13.5 1.0 constant_dynamic-slice_fusion.2
  14.6 0.3 copy.76
  14.9 0.1 collective-permute-start
  15.0 0.3 copy_dynamic-update-slice_fusion
  15.3 55.5 %fusion.37 = f32[8,8]{1,0:T(8,128)} fusion(f32[8,128,4,1024]{3,2,1,0:T(4,128)} %param.16), kind=kOutput, calls=%fused_computation.41 | convolution fusion | flops 402653184 | bytes 16777472 | tf_op jit(solution)/shard_map/japb,kapb->jk/dot_general | solution.py:46
  70.8 11.1 %collective-permute-done = bf16[128,4,1024]{2,0,1:T(8,128)(2,1)S(1)} collective-permute-done((bf16[128,4,1024]{2,0,1:T(8,128)(2,1)S(1)}, bf16[128,4,1024]{2,0,1:T(8,128)(2,1)S(1)}, u32[]{:S(2)}, u32[]{:S(2)}) %collective-permute-start) | collective-permute-done | bytes 1048608 | tf_op jit(solution)/shard_map/ppermute | solution.py:40
  81.9 0.1 constant_dynamic-update-slice_fusion
  81.9 0.0 copy-start.4
  81.9 1.6 fusion.53
  83.5 0.0 collective-permute-done.1
  83.5 0.8 copy-done.4
  84.3 4.7 pad_maximum_fusion
  89.0 50.7 %all-gather.9.cloned.1.call-done = bf16[1,2048,4,1024]{3,2,0,1:T(4,128)(2,1)} async-done(((bf16[1,128,4,1024]{3,2,0,1:T(4,128)(2,1)}), bf16[1,2048,4,1024]{3,2,0,1:T(4,128)(2,1)}) %all-gather.9.cloned.1.call-update) | async-done | bytes 16777232 | tf_op jit(solution)/shard_map/all_gather | solution.py:34
  139.7 0.0 all-gather.5.cloned.1.call-update
  139.8 0.0 all-gather.7.cloned.1.call-start
  139.8 0.2 convolution_bitcast_fusion.1
  140.0 0.0 copy-done
  140.0 0.2 convolution_bitcast_fusion
  140.2 0.6 copy.43
  140.9 0.0 copy-start.5
  141.0 0.7 slice_maximum_fusion
  141.7 17.5 %copy.85 = bf16[256,8,4,1024]{3,1,2,0:T(8,128)(2,1)} copy(bf16[256,8,4,1024]{3,2,1,0:T(4,128)(2,1)} %bitcast.147) | data formatting | bytes 33554432
  159.2 0.0 copy-done.7
  159.2 22.5 %copy.40 = bf16[4096,2048]{1,0:T(8,128)(2,1)} copy(bf16[4096,2048]{0,1:T(8,128)(2,1)} %bitcast.146) | data formatting | bytes 33554432 | tf_op jit(solution)/shard_map/dot_general | solution.py:58
  181.8 0.0 all-gather.7.cloned.1.call-update
  181.8 0.0 copy-start.6
  181.8 0.0 copy-start.8
  181.8 0.0 copy-start.9
  181.8 0.0 copy-start.10
  181.8 23.7 %fusion.15 = f32[128,8,4,1024]{3,1,2,0:T(8,128)} fusion(bf16[4,1024,2048,1]{2,1,0,3:T(8,128)(2,1)} %bitcast.148, bf16[128,8,2048]{2,1,0:T(8,128)(2,1)} %pad_maximum_fusion), kind=kOutput, calls=%fused_computation.14 | convolution fusion | flops 17179869184 | bytes 37748736 | tf_op jit(solution)/shard_map/dot_general | solution.py:58
  205.6 20.7 %fusion.12 = bf16[128,4,8,1024]{3,2,1,0:T(8,128)(2,1)} fusion(f32[128,8,4,1024]{3,1,2,0:T(8,128)} %fusion.15, f32[8,8,4,4]{1,0,3,2:T(8,128)S(1)} %bitcast.152, f32[4,8,4,4]{1,0,3,2:T(4,128)S(1)} %copy-done.8, f32[4,8,4,4]{1,0,3,2:T(4,128)S(1)} %copy-done.6, f32[8,4,4,4]{1,0,3,2:T(8,128)S(1)} %copy-done.10, pred[]{:T(512)S(6)} %eq.16), kind=kOutput, calls=%fused_computation.12 | convolution fusion | flops 1614810112 | bytes 25176064 | tf_op jit(solution)/shard_map/kypq,akqb->apyb/dot_general | solution.py:64
  226.2 40.4 %all-gather.5.cloned.1.call-done = bf16[1024,8,1024]{2,0,1:T(8,128)(2,1)} async-done(((bf16[64,8,1024]{2,0,1:T(8,128)(2,1)}), bf16[1024,8,1024]{2,0,1:T(8,128)(2,1)}) %all-gather.5.cloned.1.call-update) | async-done | bytes 16777232 | tf_op jit(solution)/shard_map/all_gather | solution.py:56
  266.6 42.4 %fusion.27 = f32[128,4,1024]{2,0,1:T(8,128)S(1)} fusion(bf16[1024,8,1024]{2,0,1:T(8,128)(2,1)} %all-gather.5.cloned.1.call-done, bf16[128,4,8,1024]{3,2,1,0:T(8,128)(2,1)} %fusion.12), kind=kOutput, calls=%fused_computation.37 | convolution fusion | flops 8589934592 | bytes 27262976 | tf_op jit(solution)/shard_map/dot_general | solution.py:70
  309.0 0.1 constant_dynamic-slice_fusion.1
  309.1 1.5 collective-permute-start.2
  310.6 83.4 %all-gather.7.cloned.1.call-done = bf16[1024,8,1024]{2,0,1:T(8,128)(2,1)} async-done(((bf16[64,8,1024]{2,0,1:T(8,128)(2,1)}), bf16[1024,8,1024]{2,0,1:T(8,128)(2,1)}) %all-gather.7.cloned.1.call-update) | async-done | bytes 16777232 | tf_op jit(solution)/shard_map/all_gather | solution.py:56
  394.0 26.9 %fusion.32 = f32[128,4,1024]{2,0,1:T(8,128)} fusion(bf16[1024,8,1024]{2,0,1:T(8,128)(2,1)} %all-gather.7.cloned.1.call-done, bf16[128,4,8,1024]{3,2,1,0:T(8,128)(2,1)} %fusion.12), kind=kOutput, calls=%fused_computation.38 | convolution fusion | flops 8589934592 | bytes 27262976 | tf_op jit(solution)/shard_map/dot_general | solution.py:70
  420.9 2.3 constant_dynamic-slice_fusion
  423.2 1.5 collective-permute-start.3
  425.3 0.0 collective-permute-done.2
  425.3 1.8 dynamic-slice_add_fusion.1
  427.1 0.3 copy.50
  427.4 21.4 %collective-permute-done.3 = f32[128,4,512]{2,0,1:T(8,128)} collective-permute-done((f32[128,4,512]{2,0,1:T(8,128)}, f32[128,4,512]{2,0,1:T(8,128)}, u32[]{:S(2)}, u32[]{:S(2)}) %collective-permute-start.3) | collective-permute-done | bytes 1048608 | tf_op jit(solution)/shard_map/ppermute | solution.py:81
  448.8 1.7 dynamic-slice_add_fusion
  450.6 0.3 copy.52
  450.9 2.4 multiply_reduce_fusion.1
  453.3 2.5 copy.61
  455.9 7.7 %multiply_reduce_fusion = f32[8]{0:T(128)S(1)} fusion(f32[8,128,4,1024]{3,2,1,0:T(4,128)} %param.16, f32[128,4,1024]{2,1,0:T(4,128)S(1)} %copy.61), kind=kLoop, calls=%fused_computation.9 | loop fusion | flops 8388600 | bytes 18874400 | tf_op jit(solution)/shard_map/reduce_sum | solution.py:86
  463.6 38.6 %all-reduce = (f32[]{:T(128)}, f32[8]{0:T(128)S(1)}, f32[8,8]{1,0:T(8,128)S(1)}) all-reduce(f32[]{:T(128)} %get-tuple-element.44, f32[8]{0:T(128)S(1)} %multiply_reduce_fusion, f32[8,8]{1,0:T(8,128)S(1)} %copy-done.11), channel_id=1, replica_groups=mesh['blk'=16,'cuts'=2] {'blk','cuts'}, use_global_device_ids=true, to_apply=%region_4.5 | all-reduce | flops 73 | bytes 584 | tf_op jit(solution)/shard_map/psum | solution.py:87
  502.2 0.6 fusion.57
  502.8 0.9 multiply_reduce_fusion.4
  503.7 0.7 fusion.56
  504.4 0.7 multiply_reduce_fusion.5
  505.1 0.7 fusion.55
  509.6 0.7 multiply_reduce_fusion.2
  515.4 0.0 copy-start.1
  515.4 13.1 %fusion.21 = f32[128,4,1024]{2,1,0:T(4,128)} fusion(f32[128,4,1024]{2,1,0:T(4,128)S(1)} %copy.61, f32[8,128,4,1024]{3,2,1,0:T(4,128)} %param.16, f32[]{:T(128)} %sqrt.3, f32[]{:T(128)} %bitcast.41, f32[]{:T(128)} %bitcast.40, f32[]{:T(128)} %bitcast.38, f32[]{:T(128)} %bitcast.37, f32[]{:T(128)} %bitcast.36, f32[]{:T(128)} %bitcast.35, f32[]{:T(128)} %bitcast.34, ...), kind=kLoop, calls=%fused_computation.22 | loop fusion | flops 8912896 | bytes 20971556 | tf_op jit(solution)/shard_map/div | solution.py:117
  (24 shorter events, 0.1 us)
Async XLA Ops:
  7.2 132.9 %copy-start = (f32[8,8,2,2]{1,3,2,0:T(2,128)S(1)}, f32[8,8,2,2]{1,3,2,0:T(2,128)}, u32[]{:S(2)}) copy-start(f32[8,8,2,2]{1,3,2,0:T(2,128)} %param.14) | copy-start | bytes 3076
  7.2 6.4 %copy-start.2 = (bf16[128,4,2048]{2,1,0:T(4,128)(2,1)S(1)}, bf16[128,4,2048]{2,1,0:T(4,128)(2,1)}, u32[]{:S(2)}) copy-start(bf16[128,4,2048]{2,1,0:T(4,128)(2,1)} %param.12) | copy-start | bytes 6291460
  7.2 132.5 %all-gather.9.cloned.1.call-start = ((), (), s32[]{:S(2)}) async-start(), calls=%async_computation.2 | async-start | bytes 17825792 | tf_op jit(solution)/shard_map/all_gather | solution.py:34
  10.4 256.1 %all-gather.5.cloned.1.call-start = ((), (), s32[]{:S(2)}) async-start(), calls=%async_computation | async-start | bytes 17825792 | tf_op jit(solution)/shard_map/all_gather | solution.py:56
  10.5 73.0 %collective-permute-start.1 = (bf16[128,4,2048]{2,1,0:T(4,128)(2,1)}, bf16[128,4,2048]{2,1,0:T(4,128)(2,1)}, u32[]{:S(2)}, u32[]{:S(2)}) collective-permute-start(bf16[128,4,2048]{2,1,0:T(4,128)(2,1)} %param.11), channel_id=1, source_target_pairs={{0,1},{1,0},{2,3},{3,2},{4,5},{5,4},{6,7},{7,6},{8,9},{9,8},{10,11... | collective-permute-start | bytes 6291464 | tf_op jit(solution)/shard_map/ppermute | solution.py:37
  14.9 67.0 %collective-permute-start = (bf16[128,4,1024]{2,0,1:T(8,128)(2,1)S(1)}, bf16[128,4,1024]{2,0,1:T(8,128)(2,1)S(1)}, u32[]{:S(2)}, u32[]{:S(2)}) collective-permute-start(bf16[128,4,1024]{2,0,1:T(8,128)(2,1)S(1)} %copy.76), channel_id=1, source_target_pairs={{0,1},{1,0},{2,3},{3,2},{4,5},{5,4},{6,7},{7,6},{8,9},{9,8},{10,11... | collective-permute-start | bytes 3145736 | tf_op jit(solution)/shard_map/ppermute | solution.py:40
  81.9 2.4 copy-start.4
  83.5 56.3 %copy-start.12 = (f32[8,8,2,2]{1,3,2,0:T(2,128)S(1)}, f32[8,8,2,2]{1,3,2,0:T(2,128)}, u32[]{:S(2)}) copy-start(f32[8,8,2,2]{1,3,2,0:T(2,128)} %param.13) | copy-start | bytes 3076
  83.5 56.3 %copy-start.13 = (s32[8]{0:T(128)S(1)}, s32[8]{0:T(128)}, u32[]{:S(2)}) copy-start(s32[8]{0:T(128)} %param.15) | copy-start | bytes 100
  139.8 254.2 %all-gather.7.cloned.1.call-start = ((), (), s32[]{:S(2)}) async-start(), calls=%async_computation.1 | async-start | bytes 17825792 | tf_op jit(solution)/shard_map/all_gather | solution.py:56
  140.9 18.3 %copy-start.5 = (f32[4,8,4,4]{1,0,3,2:T(4,128)}, f32[4,8,4,4]{1,0,3,2:T(4,128)S(1)}, u32[]{:S(2)}) copy-start(f32[4,8,4,4]{1,0,3,2:T(4,128)S(1)} %copy.46) | copy-start | bytes 6148
  141.0 18.3 %copy-start.7 = (f32[4,8,4,4]{1,0,3,2:T(4,128)}, f32[4,8,4,4]{1,0,3,2:T(4,128)S(1)}, u32[]{:S(2)}) copy-start(f32[4,8,4,4]{1,0,3,2:T(4,128)S(1)} %copy.47) | copy-start | bytes 6148
  181.8 23.8 %copy-start.6 = (f32[4,8,4,4]{1,0,3,2:T(4,128)S(1)}, f32[4,8,4,4]{1,0,3,2:T(4,128)}, u32[]{:S(2)}) copy-start(f32[4,8,4,4]{1,0,3,2:T(4,128)} %copy-done.5) | copy-start | bytes 6148
  181.8 23.7 %copy-start.8 = (f32[4,8,4,4]{1,0,3,2:T(4,128)S(1)}, f32[4,8,4,4]{1,0,3,2:T(4,128)}, u32[]{:S(2)}) copy-start(f32[4,8,4,4]{1,0,3,2:T(4,128)} %copy-done.7) | copy-start | bytes 6148
  181.8 23.7 %copy-start.9 = (f32[8,8,2,2,2,2]{1,0,5,4,3,2:T(8,128)S(1)}, f32[8,8,2,2,2,2]{1,0,5,4,3,2:T(8,128)}, u32[]{:S(2)}) copy-start(f32[8,8,2,2,2,2]{1,0,5,4,3,2:T(8,128)} %copy.43) | copy-start | bytes 12292
  181.8 23.7 %copy-start.10 = (f32[8,4,4,4]{1,0,3,2:T(8,128)S(1)}, f32[8,4,4,4]{1,0,3,2:T(8,128)}, u32[]{:S(2)}) copy-start(f32[8,4,4,4]{1,0,3,2:T(8,128)} %slice_maximum_fusion) | copy-start | bytes 6148
  308.9 112.0 %copy-start.3 = (f32[128,4,1024]{2,0,1:T(8,128)}, f32[128,4,1024]{2,0,1:T(8,128)S(1)}, u32[]{:S(2)}) copy-start(f32[128,4,1024]{2,0,1:T(8,128)S(1)} %fusion.27) | copy-start | bytes 6291460
  309.1 116.3 %collective-permute-start.2 = (f32[128,4,512]{2,0,1:T(8,128)S(1)}, f32[128,4,512]{2,0,1:T(8,128)}, u32[]{:S(2)}, u32[]{:S(2)}) collective-permute-start(f32[128,4,512]{2,0,1:T(8,128)S(1)} %constant_dynamic-slice_fusion.1), channel_id=1, source_target_pairs={{0,1},{1,0},{2,3},{3,2},{4,5},{5,4},{6,7},{7,6},{8,9},{9,8},{10,11... | collective-permute-start | bytes 3145736 | tf_op jit(solution)/shard_map/ppermute | solution.py:81
  423.2 25.6 %collective-permute-start.3 = (f32[128,4,512]{2,0,1:T(8,128)}, f32[128,4,512]{2,0,1:T(8,128)}, u32[]{:S(2)}, u32[]{:S(2)}) collective-permute-start(f32[128,4,512]{2,0,1:T(8,128)} %constant_dynamic-slice_fusion), channel_id=1, source_target_pairs={{0,1},{1,0},{2,3},{3,2},{4,5},{5,4},{6,7},{7,6},{8,9},{9,8},{10,11... | collective-permute-start | bytes 3145736 | tf_op jit(solution)/shard_map/ppermute | solution.py:81
  455.9 7.8 %copy-start.11 = (f32[8,8]{1,0:T(8,128)S(1)}, f32[8,8]{1,0:T(8,128)}, u32[]{:S(2)}) copy-start(f32[8,8]{1,0:T(8,128)} %fusion.37) | copy-start | bytes 772
  515.4 13.1 %copy-start.1 = (f32[8,8,2,2]{1,3,2,0:T(2,128)S(1)}, f32[8,8,2,2]{1,3,2,0:T(2,128)}, u32[]{:S(2)}) copy-start(f32[8,8,2,2]{1,3,2,0:T(2,128)} %param.14) | copy-start | bytes 3076
Sparse Core Ops, SparseCore 0:
  10.6 129.1 all-gather.8
  141.9 124.6 all-gather.4
  269.3 124.6 all-gather.6
